TPU v7x, 128 devices: a whole 4x4x4 slice. The times are simulated.
128 devices in a mesh: blk: 32 (over z, x, core), col: 4 (over y).
Axes of the slice: x: 4, y: 4, z: 4, core: 2. Of those that a mesh axis runs over, the one named last changes fastest.
Arguments:
- pixel_row: int32 [32768, 256], P(('blk', 'col')), may hold values from 0 to 63, as said below
- pixel_col: int32 [32768, 256], P(('blk', 'col')), may hold values from 0 to 2047, as said below
- strip_of_span: int32 [128, 256], P(('blk', 'col')), may hold values from 0 to 127, as said below
- shear_one: float32 [32768, 256], P(('blk', 'col')), may hold values from -6 to 6
- shear_two: float32 [32768, 256], P(('blk', 'col')), may hold values from -6 to 6
- weight: float32 [32768, 256], P(('blk', 'col')), may hold values from 0.25 to 4
Outputs:
- kappa_e: float32 [8192, 8192], P(('blk', 'col'))
- kappa_b: float32 [8192, 8192], P(('blk', 'col'))
Inputs may be any that keep to these rules, and one draw needn't show every extreme that they name: `pixel_row`: all galaxies of one span (one row) lie in one aligned band of 8 rows. `pixel_col`: all galaxies of one span (one row) lie in one aligned block of 128 columns. `strip_of_span`: row d names the row strip of each span of shard d; each strip is named exactly 2 times in every row.
All inputs are finite; a program needn't handle non-finite values.
Results may differ from a plain program's by a relative error of at most 0.0038.
Values may be sent and summed in bfloat16 or wider, within the bound.
No kernel may reach another device: no remote copies, remote signals or barrier semaphores. Data moves between devices by JAX's collectives and lax.ppermute only.
A program may use at most 128 MiB of HBM per device.

v0:
```python
import math

import jax
import jax.numpy as jnp
from jax import lax
from jax.sharding import PartitionSpec as P

SLAB = 256
TILE_COLS = 2048
BAND = 8
SUBC = 128
DEPTH = 2


highest = lax.Precision.HIGHEST


def factor_pair(length):
    return (length // 128, 128)


def complex_table(left_len, right_len, modulus, direction):
    first_idx = lax.broadcasted_iota(jnp.int32, (left_len, right_len), 0)
    second_idx = lax.broadcasted_iota(jnp.int32, (left_len, right_len), 1)
    angles = (
        direction * 2.0 * math.pi / modulus * (first_idx * second_idx % modulus).astype(jnp.float32)
    )
    cosine = jnp.cos(angles)
    sine_part = jnp.sin(angles)
    return jnp.stack([jnp.stack([cosine, sine_part], -1), jnp.stack([-sine_part, cosine], -1)], 0)


def twiddle_parts(outer_len, inner_len, modulus, direction, factor):
    first_idx = lax.broadcasted_iota(jnp.int32, (outer_len, inner_len), 0)
    second_idx = lax.broadcasted_iota(jnp.int32, (outer_len, inner_len), 1)
    angles = (
        direction * 2.0 * math.pi / modulus * (first_idx * second_idx % modulus).astype(jnp.float32)
    )
    return (factor * jnp.cos(angles), factor * jnp.sin(angles))


def rotate(complex_field, cosine, sine_part):
    return jnp.stack(
        [
            complex_field[0] * cosine - complex_field[1] * sine_part,
            complex_field[0] * sine_part + complex_field[1] * cosine,
        ]
    )


def transform_rows(complex_field, direction):
    row_count = complex_field.shape[1]
    length = complex_field.shape[2]
    outer_len, inner_len = factor_pair(length)
    factor = 1.0 if direction < 0 else 1.0 / length
    cosine, sine_part = twiddle_parts(outer_len, inner_len, length, direction, factor)
    small_table = complex_table(outer_len, outer_len, outer_len, direction)
    large_table = complex_table(inner_len, inner_len, inner_len, direction)
    blocked = complex_field.reshape(2, row_count, outer_len, inner_len)
    if direction < 0:
        blocked = jnp.einsum("prab,pakq->qrkb", blocked, small_table, precision=highest)
        blocked = rotate(blocked, cosine, sine_part)
        blocked = jnp.einsum("prkb,pbsq->qrks", blocked, large_table, precision=highest)
    else:
        blocked = jnp.einsum("prks,psbq->qrkb", blocked, large_table, precision=highest)
        blocked = rotate(blocked, cosine, sine_part)
        blocked = jnp.einsum("prkb,pkaq->qrab", blocked, small_table, precision=highest)
    return blocked.reshape(2, row_count, length)


def transform_columns(complex_field, direction):
    length = complex_field.shape[1]
    col_count = complex_field.shape[2]
    outer_len, inner_len = factor_pair(length)
    factor = 1.0 if direction < 0 else 1.0 / length
    cosine, sine_part = twiddle_parts(outer_len, inner_len, length, direction, factor)
    cosine = cosine[:, :, None]
    sine_part = sine_part[:, :, None]
    small_table = complex_table(outer_len, outer_len, outer_len, direction)
    large_table = complex_table(inner_len, inner_len, inner_len, direction)
    blocked = complex_field.reshape(2, outer_len, inner_len, col_count)
    if direction < 0:
        blocked = jnp.einsum("pabw,pakq->qkbw", blocked, small_table, precision=highest)
        blocked = rotate(blocked, cosine, sine_part)
        blocked = jnp.einsum("pkbw,pbsq->qksw", blocked, large_table, precision=highest)
    else:
        blocked = jnp.einsum("pksw,psbq->qkbw", blocked, large_table, precision=highest)
        blocked = rotate(blocked, cosine, sine_part)
        blocked = jnp.einsum("pkbw,pkaq->qabw", blocked, small_table, precision=highest)
    return blocked.reshape(2, length, col_count)


def signed_frequency(position, length):
    outer_len, inner_len = factor_pair(length)
    freq_index = position // inner_len + outer_len * (position % inner_len)
    signed = jnp.where(freq_index < length // 2, freq_index, freq_index - length)
    return signed.astype(jnp.float32) / length


def bin_region(rows_in, cols_in, values, region_rows, region_cols):
    span_count = rows_in.shape[0]
    galaxies = rows_in.shape[1]
    band_count = region_rows // BAND
    blocks = region_cols // SUBC
    position = rows_in[:, 0] // BAND * blocks + cols_in[:, 0] // SUBC
    group_size = math.gcd(span_count, 128)

    def one_group(unused, group_data):
        row_part, col_part, value_part = group_data
        row_hot = (row_part[:, None, :] == lax.broadcasted_iota(jnp.int32, (1, BAND, 1), 1)).astype(
            jnp.bfloat16
        )
        weighted = (value_part[:, :, None, :] * row_hot[:, None, :, :]).reshape(
            group_size, 3 * BAND, galaxies
        )
        col_hot = (col_part[:, :, None] == lax.broadcasted_iota(jnp.int32, (1, 1, SUBC), 2)).astype(
            jnp.bfloat16
        )
        return (
            unused,
            jnp.einsum("ckg,cgs->cks", weighted, col_hot, preferred_element_type=jnp.float32),
        )

    group_inputs = (
        (rows_in % BAND).reshape(-1, group_size, galaxies),
        (cols_in % SUBC).reshape(-1, group_size, galaxies),
        values.reshape(-1, group_size, 3, galaxies),
    )
    unused_carry, partials = lax.scan(one_group, jnp.zeros((), jnp.float32), group_inputs)
    partials = partials.reshape(span_count, 3 * BAND * SUBC)
    summed = jax.ops.segment_sum(partials, position, num_segments=band_count * blocks)
    summed = summed.reshape(band_count, blocks, 3, BAND, SUBC).transpose(2, 0, 3, 1, 4)
    summed = summed.reshape(3, region_rows, region_cols)
    floored = jnp.maximum(summed[0], 1.0)
    return jnp.stack([summed[1] / floored, summed[2] / floored])


def local(pixel_row, pixel_col, strip_of_span, shear_one, shear_two, weight):
    tile_count = lax.axis_size("col")
    my_slab = lax.axis_index("blk")
    my_tile = lax.axis_index("col")
    strip_rows = SLAB // tile_count
    span_total = pixel_row.shape[0]
    by_strip = jnp.argsort(strip_of_span[0], stable=True)
    packed = jnp.take(pixel_row * TILE_COLS + pixel_col, by_strip, axis=0)
    values = jnp.stack(
        [
            weight.astype(jnp.bfloat16),
            (weight * shear_one).astype(jnp.bfloat16),
            (weight * shear_two).astype(jnp.bfloat16),
        ],
        axis=1,
    )
    values = jnp.take(values, by_strip, axis=0)
    arrival = jnp.arange(span_total, dtype=jnp.int32) // DEPTH
    own_cell, own_values = (
        lax.all_to_all(packed, ("blk", "col"), split_axis=0, concat_axis=0, tiled=True),
        lax.all_to_all(values, ("blk", "col"), split_axis=0, concat_axis=0, tiled=True),
    )
    rows_in = own_cell // TILE_COLS
    cols_in = (arrival % tile_count)[:, None] * TILE_COLS + own_cell % TILE_COLS
    whole_rows = bin_region(rows_in, cols_in, own_values, strip_rows, TILE_COLS * tile_count)
    row_spectrum = transform_rows(whole_rows, -1)
    total_cols = row_spectrum.shape[2]
    whole_cols = lax.all_to_all(
        row_spectrum, ("blk", "col"), split_axis=2, concat_axis=1, tiled=True
    )
    col_width = whole_cols.shape[2]
    first_col = (my_slab * tile_count + my_tile) * col_width
    spectrum = transform_columns(whole_cols, -1)
    total_rows = spectrum.shape[1]
    freq_y = signed_frequency(jnp.arange(total_rows, dtype=jnp.int32), total_rows)[:, None]
    freq_x = signed_frequency(first_col + jnp.arange(col_width, dtype=jnp.int32), total_cols)[
        None, :
    ]
    radius_sq = freq_x * freq_x + freq_y * freq_y
    safe_radius = jnp.where(radius_sq > 0, radius_sq, 1.0)
    kernel_re = (freq_x * freq_x - freq_y * freq_y) / safe_radius
    kernel_im = 2.0 * freq_x * freq_y / safe_radius
    kappa_hat = jnp.stack(
        [
            kernel_re * spectrum[0] + kernel_im * spectrum[1],
            kernel_re * spectrum[1] - kernel_im * spectrum[0],
        ]
    )
    col_result = transform_columns(kappa_hat, 1)
    back_rows = lax.all_to_all(col_result, ("blk", "col"), split_axis=1, concat_axis=2, tiled=True)
    convergence = transform_rows(back_rows, 1)
    return (convergence[0], convergence[1])


def solution(mesh):
    placed = (
        P(("blk", "col"), None),
        P(("blk", "col"), None),
        P(("blk", "col"), None),
        P(("blk", "col"), None),
        P(("blk", "col"), None),
        P(("blk", "col"), None),
    )
    return jax.shard_map(
        local,
        mesh=mesh,
        in_specs=placed,
        out_specs=(P(("blk", "col"), None), P(("blk", "col"), None)),
        check_vma=False,
    )
```

profile of v0, /device:TPU:1, one launch (start us, length us, event | category | flops | bytes accessed | tf_op | source)
XLA Modules:
  0.0 376.3 jit_solution(13310990043831622267)
XLA Ops:
  0.6 3.8 %sort.17 = (s32[256]{0:T(256)}, s32[256]{0:T(256)S(1)}) sort(s32[256]{0:T(256)} %bitcast.215, s32[256]{0:T(256)S(1)} %iota.347), dimensions={0}, to_apply=%region_0.0 | sort | flops 2048 | bytes 4096 | tf_op jit(solution)/shard_map/jit(argsort)/sort | solution.py:144
  7.8 11.5 %all-to-all-start = ((s32[128,2,256]{2,1,0:T(2,128)}), s32[128,2,256]{2,1,0:T(2,128)S(1)}, u32[]{:S(2)}, u32[]{:S(2)}) async-start(s32[128,2,256]{2,1,0:T(2,128)} %broadcast_select_fusion.1), calls=%async_computation | async-start | bytes 524288 | tf_op jit(solution)/shard_map/all_to_all | solution.py:157
  24.9 5.4 %all-to-all-done = s32[128,2,256]{2,1,0:T(2,128)S(1)} async-done(((s32[128,2,256]{2,1,0:T(2,128)}), s32[128,2,256]{2,1,0:T(2,128)S(1)}, u32[]{:S(2)}, u32[]{:S(2)}) %all-to-all-start) | async-done | bytes 262176 | tf_op jit(solution)/shard_map/all_to_all | solution.py:157
  30.3 4.6 %all-to-all-start.1 = ((bf16[256,3,256]{2,1,0:T(4,128)(2,1)}), bf16[256,3,256]{2,1,0:T(4,128)(2,1)S(1)}, u32[]{:S(2)}, u32[]{:S(2)}) async-start(bf16[256,3,256]{2,1,0:T(4,128)(2,1)} %broadcast_select_fusion), calls=%async_computation.1 | async-start | bytes 1048576 | tf_op jit(solution)/shard_map/all_to_all | solution.py:158
  36.2 12.4 %all-to-all-done.1 = bf16[256,3,256]{2,1,0:T(4,128)(2,1)S(1)} async-done(((bf16[256,3,256]{2,1,0:T(4,128)(2,1)}), bf16[256,3,256]{2,1,0:T(4,128)(2,1)S(1)}, u32[]{:S(2)}, u32[]{:S(2)}) %all-to-all-start.1) | async-done | bytes 393248 | tf_op jit(solution)/shard_map/all_to_all | solution.py:158
  48.6 17.0 %while.10 = (s32[]{:T(128)}, f32[2,128,24,128]{3,2,1,0:T(8,128)}, bf16[2,128,3,256]{3,2,1,0:T(4,128)(2,1)S(1)}, s32[2,128,256]{2,1,0:T(8,128)S(1)}, s32[2,128,256]{2,1,0:T(8,128)S(1)}, /*index=5*/s32[]{:T(128)}) while((s32[]{:T(128)}, f32[2,128,24,128]{3,2,1,0:T(8,128)}, bf16[2,128,3,256]{3,2,1,0:T(4,128)(2,1)S(1)}, ...), condition=%wide.region_2.3_spmd, body=%wide.region_1.2_spmd.sunk | while | flops 206831616 | bytes 3998285 | solution.py:129
  48.8 8.3 %bitcast_dynamic-update-slice_fusion.2 = f32[2,128,24,128]{3,2,1,0:T(8,128)} fusion(f32[2,128,24,128]{3,2,1,0:T(8,128)} %get-tuple-element.133, s32[]{:T(128)} %get-tuple-element.132, s32[128,256]{1,0:T(8,128)S(1)} %get-tuple-element.124, bf16[128,8,256]{2,1,0:T(8,128)(2,1)S(1)} %fusion.125, bf16[128,3,256]{2,1,0:T(4,128)(2,1)S(1)} %dynamic-slice_bitcast_fusion.6), kind=kOutput, calls=%fused_computation.6.clone.1 | convolution fusion | flops 206307328 | bytes 2425344 | tf_op jit(solution)/shard_map/while/body/eval_jaxpr/ckg,cgs->cks/dot_general | solution.py:121
  57.3 8.3 %bitcast_dynamic-update-slice_fusion.2 = f32[2,128,24,128]{3,2,1,0:T(8,128)} fusion(f32[2,128,24,128]{3,2,1,0:T(8,128)} %get-tuple-element.133, s32[]{:T(128)} %get-tuple-element.132, s32[128,256]{1,0:T(8,128)S(1)} %get-tuple-element.124, bf16[128,8,256]{2,1,0:T(8,128)(2,1)S(1)} %fusion.125, bf16[128,3,256]{2,1,0:T(4,128)(2,1)S(1)} %dynamic-slice_bitcast_fusion.6), kind=kOutput, calls=%fused_computation.6.clone.1 | convolution fusion | flops 206307328 | bytes 2425344 | tf_op jit(solution)/shard_map/while/body/eval_jaxpr/ckg,cgs->cks/dot_general | solution.py:121
  65.6 9.8 %scatter_custom_fusion = f32[512,3072]{1,0:T(8,128)} fusion(s32[256]{0:T(256)S(1)} %fusion.70, f32[32,8,24,128]{3,2,1,0:T(8,128)} %bitcast.212, f32[]{:T(128)} %constant.283.clone.1), kind=kCustom, calls=%fused_computation.49 | custom fusion | flops 786432 | bytes 9437188 | tf_op jit(solution)/shard_map/scatter-add | solution.py:131
  75.4 4.2 %copy.112 = f32[64,8,24,128]{3,2,1,0:T(8,128)S(1)} copy(f32[64,8,24,128]{3,1,2,0:T(8,128)} %bitcast.205) | data formatting | bytes 12582912
  80.6 3.9 %fusion.58 = f32[2,64,64,128]{3,2,1,0:T(8,128)S(1)} fusion(f32[1,64,64,128]{3,2,0,1:T(8,128)S(1)} %bitcast.209, f32[1,64,64,128]{3,2,0,1:T(8,128)S(1)} %bitcast.207, f32[1,64,64,2]{1,2,0,3:T(8,128)S(1)} %get-tuple-element.74, f32[1,64,64,2]{1,2,0,3:T(8,128)S(1)} %get-tuple-element.73), kind=kOutput, calls=%fused_computation.60 | convolution fusion | flops 1611677696 | bytes 8454144 | tf_op jit(solution)/shard_map/prab,pakq->qrkb/dot_general | solution.py:61
  85.5 5.1 %fusion.37 = f32[2,64,64,128]{3,2,1,0:T(8,128)} fusion(f32[1,128,128,2]{2,1,0,3:T(8,128)S(1)} %get-tuple-element.70, f32[1,128,128,2]{2,1,0,3:T(8,128)S(1)} %get-tuple-element.69, f32[1,64,64,128]{3,2,1,0:T(8,128)S(1)} %get-tuple-element.59, f32[1,64,64,128]{3,2,1,0:T(8,128)S(1)} %get-tuple-element.58), kind=kOutput, calls=%fused_computation.53 | convolution fusion | flops 3222339584 | bytes 8650752 | tf_op jit(solution)/shard_map/prkb,pbsq->qrks/dot_general | solution.py:63
  90.5 8.4 %copy.105 = f32[2,64,64,128]{1,0,3,2:T(2,128)} copy(f32[2,64,64,128]{3,2,1,0:T(8,128)} %fusion.37) | data formatting | bytes 8388608 | tf_op jit(solution)/shard_map/reshape | solution.py:68
  98.9 11.1 %reshape.668 = f32[128,1,8192]{2,1,0:T(1,128)} reshape(f32[8192,2,64]{2,1,0:T(2,128)} %bitcast.199) | data formatting | bytes 8388608
  110.0 5.5 %all-to-all-start.2 = ((f32[128,1,8192]{2,1,0:T(1,128)}), f32[128,1,8192]{2,1,0:T(1,128)}, u32[]{:S(2)}, u32[]{:S(2)}) async-start(f32[128,1,8192]{2,1,0:T(1,128)} %reshape.668), calls=%async_computation.2 | async-start | bytes 8388608 | tf_op jit(solution)/shard_map/all_to_all | solution.py:165
  116.7 51.7 %all-to-all-done.2 = f32[128,1,8192]{2,1,0:T(1,128)} async-done(((f32[128,1,8192]{2,1,0:T(1,128)}), f32[128,1,8192]{2,1,0:T(1,128)}, u32[]{:S(2)}, u32[]{:S(2)}) %all-to-all-start.2) | async-done | bytes 4194336 | tf_op jit(solution)/shard_map/all_to_all | solution.py:165
  168.9 13.8 %reduce.2 = f32[128,8192]{1,0:T(8,128)} reduce(f32[128,1,8192]{2,1,0:T(1,128)} %all-to-all-done.2, f32[]{:T(128)} %broadcast.1207), dimensions={1}, to_apply=%all_to_all.37.reduce_sub_computation | reduce | bytes 8388612 | tf_op jit(solution)/shard_map/all_to_all | solution.py:165
  182.7 9.6 %reshape.669 = f32[8192,2,64]{2,1,0:T(2,128)} reshape(f32[128,8192]{1,0:T(8,128)} %reduce.2) | data formatting | bytes 8388608
  192.3 11.5 %copy.174 = f32[2,64,128,64]{1,2,3,0:T(8,128)} copy(f32[2,64,128,64]{1,0,3,2:T(2,128)} %bitcast.201) | data formatting | bytes 8388608 | tf_op jit(solution)/shard_map/all_to_all | solution.py:165
  203.7 7.2 %reshape.614 = f32[2,64,128,64]{2,1,3,0:T(8,128)} reshape(f32[2,128,64,64]{2,1,3,0:T(8,128)} %bitcast.202) | data formatting | bytes 8388608 | tf_op jit(solution)/shard_map/reshape | solution.py:81
  211.0 5.7 %fusion.40 = f32[2,64,128,64]{2,1,3,0:T(8,128)S(1)} fusion(f32[2,64,128,64]{2,1,3,0:T(8,128)} %reshape.614, f32[1,64,64,2]{1,2,0,3:T(8,128)S(1)} %get-tuple-element.74, f32[1,64,64,2]{1,2,0,3:T(8,128)S(1)} %get-tuple-element.73), kind=kOutput, calls=%fused_computation.54 | convolution fusion | flops 1610629120 | bytes 8454144 | tf_op jit(solution)/shard_map/pabw,pakq->qkbw/dot_general | solution.py:83
  218.2 6.6 %fusion.43 = f32[2,64,128,64]{2,3,1,0:T(8,128)S(1)} fusion(f32[2,64,128,64]{2,1,3,0:T(8,128)S(1)} %pad_maximum_fusion.1, f32[1,128,128,2]{2,1,0,3:T(8,128)S(1)} %get-tuple-element.70, f32[1,128,128,2]{2,1,0,3:T(8,128)S(1)} %get-tuple-element.69), kind=kOutput, calls=%fused_computation.55 | convolution fusion | flops 3221291008 | bytes 8650752 | tf_op jit(solution)/shard_map/pkbw,pbsq->qksw/dot_general | solution.py:85
  231.2 9.0 %fusion.49 = f32[2,64,128,64]{2,1,3,0:T(8,128)} fusion(f32[2,64,128,64]{2,3,1,0:T(8,128)S(1)} %pad_maximum_fusion.3, f32[1,64,64,2]{1,2,3,0:T(8,128)S(1)} %get-tuple-element.72, f32[1,64,64,2]{1,2,3,0:T(8,128)S(1)} %get-tuple-element.71), kind=kOutput, calls=%fused_computation.57 | convolution fusion | flops 1610629120 | bytes 8454144 | tf_op jit(solution)/shard_map/pkbw,pkaq->qabw/dot_general | solution.py:89
  240.2 8.4 %copy.108 = f32[2,64,128,64]{3,0,2,1:T(2,128)} copy(f32[2,64,128,64]{2,1,3,0:T(8,128)} %fusion.49) | data formatting | bytes 8388608 | tf_op jit(solution)/shard_map/reshape | solution.py:90
  248.5 11.1 %reshape.670 = f32[128,1,8192]{2,1,0:T(1,128)} reshape(f32[8192,2,64]{2,1,0:T(2,128)} %bitcast.200) | data formatting | bytes 8388608
  259.7 57.8 %all_to_all.47 = f32[128,1,8192]{2,1,0:T(1,128)} all-to-all(f32[128,1,8192]{2,1,0:T(1,128)} %reshape.670), channel_id=1, replica_groups=mesh['blk'=32,'col'=4] {'blk','col'}, dimensions={0} | all-to-all | bytes 8388608 | tf_op jit(solution)/shard_map/all_to_all | solution.py:187
  317.5 13.8 %reduce.3 = f32[128,8192]{1,0:T(8,128)} reduce(f32[128,1,8192]{2,1,0:T(1,128)} %all_to_all.47, f32[]{:T(128)} %broadcast.1207), dimensions={1}, to_apply=%all_to_all.40.reduce_sub_computation | reduce | bytes 8388612 | tf_op jit(solution)/shard_map/all_to_all | solution.py:187
  331.3 9.6 %reshape.671 = f32[8192,2,64]{2,1,0:T(2,128)} reshape(f32[128,8192]{1,0:T(8,128)} %reduce.3) | data formatting | bytes 8388608
  340.9 11.5 %copy.173 = f32[2,128,64,64]{3,1,2,0:T(8,128)} copy(f32[2,128,64,64]{3,0,2,1:T(2,128)} %bitcast.203) | data formatting | bytes 8388608 | tf_op jit(solution)/shard_map/all_to_all | solution.py:187
  352.3 7.2 %reshape.616 = f32[2,64,64,128]{3,2,1,0:T(8,128)} reshape(f32[2,64,128,64]{3,2,1,0:T(8,128)} %bitcast.204) | data formatting | bytes 8388608 | tf_op jit(solution)/shard_map/reshape | solution.py:59
  359.6 6.1 %fusion.52 = f32[2,64,64,128]{3,2,1,0:T(8,128)S(1)} fusion(f32[2,64,64,128]{3,2,1,0:T(8,128)} %reshape.616, f32[1,128,128,2]{2,1,3,0:T(8,128)S(1)} %get-tuple-element.68, f32[1,128,128,2]{2,1,3,0:T(8,128)S(1)} %get-tuple-element.67), kind=kOutput, calls=%fused_computation.58 | convolution fusion | flops 3221291008 | bytes 8650752 | tf_op jit(solution)/shard_map/prks,psbq->qrkb/dot_general | solution.py:65
  366.7 3.8 %fusion.55 = f32[2,64,64,128]{3,2,1,0:T(8,128)S(1)} fusion(f32[1,64,64,128]{3,2,1,0:T(8,128)S(1)} %get-tuple-element.53, f32[1,64,64,128]{3,2,1,0:T(8,128)S(1)} %get-tuple-element.52, f32[1,64,64,2]{1,2,3,0:T(8,128)S(1)} %get-tuple-element.72, f32[1,64,64,2]{1,2,3,0:T(8,128)S(1)} %get-tuple-element.71), kind=kOutput, calls=%fused_computation.59 | convolution fusion | flops 1611677696 | bytes 8454144 | tf_op jit(solution)/shard_map/prkb,pkaq->qrab/dot_general | solution.py:67
  (67 shorter events, 28.6 us)
Async XLA Ops:
  5.6 14.7 %copy-start = (f32[256,256]{1,0:T(8,128)S(1)}, f32[256,256]{1,0:T(8,128)}, u32[]{:S(2)}) copy-start(f32[256,256]{1,0:T(8,128)} %param.13) | copy-start | bytes 786436
  5.6 14.7 %copy-start.1 = (f32[256,256]{1,0:T(8,128)S(1)}, f32[256,256]{1,0:T(8,128)}, u32[]{:S(2)}) copy-start(f32[256,256]{1,0:T(8,128)} %param.12) | copy-start | bytes 786436
  5.6 14.7 %copy-start.2 = (f32[256,256]{1,0:T(8,128)S(1)}, f32[256,256]{1,0:T(8,128)}, u32[]{:S(2)}) copy-start(f32[256,256]{1,0:T(8,128)} %param.11) | copy-start | bytes 786436
  7.8 22.5 %all-to-all-start = ((s32[128,2,256]{2,1,0:T(2,128)}), s32[128,2,256]{2,1,0:T(2,128)S(1)}, u32[]{:S(2)}, u32[]{:S(2)}) async-start(s32[128,2,256]{2,1,0:T(2,128)} %broadcast_select_fusion.1), calls=%async_computation | async-start | bytes 524288 | tf_op jit(solution)/shard_map/all_to_all | solution.py:157
  30.3 18.3 %all-to-all-start.1 = ((bf16[256,3,256]{2,1,0:T(4,128)(2,1)}), bf16[256,3,256]{2,1,0:T(4,128)(2,1)S(1)}, u32[]{:S(2)}, u32[]{:S(2)}) async-start(bf16[256,3,256]{2,1,0:T(4,128)(2,1)} %broadcast_select_fusion), calls=%async_computation.1 | async-start | bytes 1048576 | tf_op jit(solution)/shard_map/all_to_all | solution.py:158
  110.0 58.4 %all-to-all-start.2 = ((f32[128,1,8192]{2,1,0:T(1,128)}), f32[128,1,8192]{2,1,0:T(1,128)}, u32[]{:S(2)}, u32[]{:S(2)}) async-start(f32[128,1,8192]{2,1,0:T(1,128)} %reshape.668), calls=%async_computation.2 | async-start | bytes 8388608 | tf_op jit(solution)/shard_map/all_to_all | solution.py:165
where the time goes:
time: 383 us; the launch traced here: 376 us
  local copies, waits for them, and re-layouts  110 us (29%)
  waiting for transfers between devices  69.5 us (18%)
  matrix products  60.3 us (16%)
  blocking collectives  57.8 us (15%)
  other arithmetic  55.6 us (15%)
  starting transfers between devices  21.6 us (6%)
    all_to_all x1, blocking collectives, local(): lax.all_to_all(col_result, ('blk', 'col'), split_axis=1, concat_axis=2, t...  57.8 us
    all_to_all x1, waiting for transfers between devices, local(): lax.all_to_all(row_spectrum, ('blk', 'col'), split_axis=2, concat_axis=1,...  51.7 us
    unnamed x13, local copies, waits for them, and re-layouts  50.6 us
    dot_general x2, matrix products, one_group(): jnp.einsum('ckg,cgs->cks', weighted, col_hot, preferred_element_type=jnp....  16.5 us
    all_to_all x1, other arithmetic, local(): lax.all_to_all(col_result, ('blk', 'col'), split_axis=1, concat_axis=2, t...  13.8 us
    all_to_all x1, other arithmetic, local(): lax.all_to_all(row_spectrum, ('blk', 'col'), split_axis=2, concat_axis=1,...  13.8 us
    all_to_all x1, waiting for transfers between devices, local(): lax.all_to_all(values, ('blk', 'col'), split_axis=0, concat_axis=0, tiled...  12.4 us
    all_to_all x2, local copies, waits for them, and re-layouts, local(): lax.all_to_all(row_spectrum, ('blk', 'col'), split_axis=2, concat_axis=1,...  12 us
  transfers between devices with their start and end apart: 3, of which 3 were waited for; matrix products, arithmetic and copies ran while one was open for 2% of the time, Pallas kernels for 0%

commit v1 on v0

v1 whole, which is shorter than its diff:
```python
import math

import jax
import jax.numpy as jnp
import numpy as np
from jax import lax
from jax.experimental import pallas as pl
from jax.experimental.pallas import tpu as pltpu
from jax.sharding import PartitionSpec as P

N = 8192
DEV = 128
F32 = jnp.float32
BF16 = jnp.bfloat16
VMEM = pl.BlockSpec(memory_space=pltpu.VMEM)
SMEM = pl.BlockSpec(memory_space=pltpu.SMEM)


def split_table(table):
    high = table.astype(BF16)
    low = (table - high.astype(np.float64)).astype(BF16)
    return jnp.asarray(high), jnp.asarray(low)


def real_form(angle):
    c, s = np.cos(angle), np.sin(angle)
    return np.stack([np.stack([c, s], 1), np.stack([-s, c], 1)], 0)


def row_table():
    b = np.arange(128)[:, None]
    q = np.arange(128)[None, :]
    m = real_form(-2 * np.pi * (b * q % 128) / 128)
    m = m.reshape(2, 128, 2, 2, 2, 32)
    return m.transpose(0, 1, 4, 3, 2, 5).reshape(256, 256)


def row_inverse_table():
    q = np.arange(128)[:, None]
    b = np.arange(128)[None, :]
    m = real_form(2 * np.pi * (b * q % 128) / 128)
    m = m.reshape(2, 2, 2, 32, 2, 128)
    return m.transpose(2, 1, 0, 3, 4, 5).reshape(256, 256)


def col_table(sign):
    b = np.arange(64)[:, None]
    q = np.arange(64)[None, :]
    m = real_form(sign * 2 * np.pi * (b * q % 64) / 64)
    full = np.zeros((2, 2, 64, 2, 2, 64))
    for par in range(2):
        full[:, par, :, :, par, :] = m
    return full.reshape(256, 256)


def twiddle_table(rows, lanes, sign, factor):
    r = np.arange(rows)[:, None]
    angle = sign * 2 * np.pi * (r * lanes[None, :] % N) / N
    return (
        jnp.asarray(factor * np.cos(angle), F32),
        jnp.asarray(factor * np.sin(angle), F32),
    )


def times(value, k, n, sign):
    re, im = value
    k = k % n
    if k == 0:
        return re, im
    if 4 * k == n:
        return (im, -re) if sign < 0 else (-im, re)
    if 2 * k == n:
        return -re, -im
    if 4 * k == 3 * n:
        return (-im, re) if sign < 0 else (im, -re)
    c = math.cos(2 * math.pi * k / n)
    s = sign * math.sin(2 * math.pi * k / n)
    if 8 * k == n or 8 * k == 5 * n or 8 * k == 3 * n or 8 * k == 7 * n:
        root = math.sqrt(0.5)
        sc = 1.0 if c > 0 else -1.0
        ss = 1.0 if s > 0 else -1.0
        if sc == ss:
            return (re - im) * (sc * root), (re + im) * (sc * root)
        return (re + im) * (sc * root), (im - re) * (sc * root)
    return re * c - im * s, re * s + im * c


def small_dft(values, sign):
    n = len(values)
    if n == 1:
        return values
    even = small_dft(values[0::2], sign)
    odd = small_dft(values[1::2], sign)
    low, high = [], []
    for k in range(n // 2):
        er, ei = even[k]
        tr, ti = times(odd[k], k, n, sign)
        low.append((er + tr, ei + ti))
        high.append((er - tr, ei - ti))
    return low + high


def major_dft(load, store, scratch, first, second, sign):
    n = first * second
    for i0 in range(second):
        out = small_dft([load(second * i1 + i0) for i1 in range(first)], sign)
        for o0 in range(first):
            re, im = times(out[o0], i0 * o0, n, sign)
            scratch[0, o0 * second + i0] = re
            scratch[1, o0 * second + i0] = im
    for o0 in range(first):
        vals = [(scratch[0, o0 * second + i0], scratch[1, o0 * second + i0]) for i0 in range(second)]
        out = small_dft(vals, sign)
        for o1 in range(second):
            store(o0 + first * o1, out[o1])


def dot(a, b):
    return jnp.dot(a, b, preferred_element_type=F32)


def dot3(x, high, low):
    xh = x.astype(BF16)
    xl = (x - xh.astype(F32)).astype(BF16)
    return dot(xh, high) + dot(xl, high) + dot(xh, low)


def pack_kernel(row_ref, col_ref, strip_ref, one_ref, two_ref, w_ref, out_ref):
    strip = strip_ref[...].astype(F32)
    along = jnp.broadcast_to(strip, (256, 256))
    down = along.T
    i = lax.broadcasted_iota(jnp.int32, (256, 256), 0)
    j = lax.broadcasted_iota(jnp.int32, (256, 256), 1)
    earlier = jnp.where((along == down) & (i < j), 1.0, 0.0)
    place = 2.0 * strip + jnp.sum(earlier, axis=0, keepdims=True)
    pick = (place.astype(jnp.int32) == i).astype(BF16)
    w = w_ref[...]
    row = row_ref[...]
    col = col_ref[...]
    block = col // 128
    a = (row * 4 + block % 4 + 1) * jnp.where(block >= 8, -1, 1)
    b = col % 128 + 128 * (block // 4 % 2)
    fields = [
        w.astype(BF16),
        (w * one_ref[...]).astype(BF16),
        (w * two_ref[...]).astype(BF16),
        a.astype(F32).astype(BF16),
        b.astype(F32).astype(BF16),
    ]
    for f in range(5):
        out_ref[:, f * 256 : (f + 1) * 256] = dot(pick, fields[f]).astype(BF16)


def row_kernel(
    band_ref, block_ref, in_ref, tc_ref, ts_ref, wh_ref, wl_ref, out_ref, acc_ref, scr_ref, mid_ref
):
    acc_ref[...] = jnp.zeros_like(acc_ref)
    lane_iota = lax.broadcasted_iota(jnp.int32, (128, 256), 0)
    row_iota = lax.broadcasted_iota(jnp.int32, (8, 256), 0)

    def bin_group(g, carry):
        start = pl.multiple_of(g * 16, 16)
        data = in_ref[pl.ds(start, 16), :].astype(F32)
        a = (jnp.abs(data[:, 768:1024]) - 1.0).astype(jnp.int32)
        row8 = (a >> 2) & 7
        col128 = data[:, 1024:1280].astype(jnp.int32) & 127
        for k in range(16):
            hot = row8[k : k + 1] == row_iota
            lhs = jnp.concatenate(
                [jnp.where(hot, data[k : k + 1, f * 256 : (f + 1) * 256], 0.0) for f in range(3)], 0
            ).astype(BF16)
            cols = jnp.where(col128[k : k + 1] == lane_iota, 1.0, 0.0).astype(BF16)
            part = lax.dot_general(lhs, cols, (((1,), (1,)), ((), ())), preferred_element_type=F32)
            band = pl.multiple_of(band_ref[start + k] * 8, 8)
            block = block_ref[start + k]
            for f in range(3):
                acc_ref[f, block, pl.ds(band, 8), :] += part[f * 8 : f * 8 + 8]
        return carry

    lax.fori_loop(0, 16, bin_group, 0)

    def row_group(g, carry):
        rows = pl.ds(pl.multiple_of(g * 8, 8), 8)

        def load(i):
            scale = 1.0 / jnp.maximum(acc_ref[0, i, rows, :], 1.0)
            return acc_ref[1, i, rows, :] * scale, acc_ref[2, i, rows, :] * scale

        def store(p, value):
            re, im = value
            c, s = tc_ref[p : p + 1, :], ts_ref[p : p + 1, :]
            mid_ref[p, rows, 0:128] = re * c - im * s
            mid_ref[p, rows, 128:256] = re * s + im * c

        major_dft(load, store, scr_ref, 8, 8, -1)
        return carry

    lax.fori_loop(0, 8, row_group, 0)

    def mix(g, carry):
        p = g * 4
        lhs = mid_ref[pl.ds(p, 4), :, :].reshape(256, 256)
        out = dot3(lhs, wh_ref[...], wl_ref[...])
        for k in range(4):
            part = out[64 * k : 64 * k + 64]
            turned = jnp.concatenate([part[:, 0:128], part[:, 128:256]], 0).T
            out_ref[pl.ds(2 * (p + k), 2), :, :] = turned.astype(BF16).reshape(2, 64, 128)
        return carry

    lax.fori_loop(0, 16, mix, 0)


def col_kernel(
    me_ref, in_ref, tc_ref, ts_ref, fh_ref, fl_ref, gh_ref, gl_ref, out_ref, scr_ref, mid_ref
):
    me = me_ref[0]

    def forward(g, carry):
        rows = pl.ds(pl.multiple_of(g * 8, 8), 8)
        rows_im = pl.ds(pl.multiple_of(g * 8 + 32, 8), 8)

        def load(i):
            return in_ref[i, rows, :].astype(F32), in_ref[i, rows_im, :].astype(F32)

        def store(p, value):
            re, im = value
            c, s = tc_ref[p : p + 1, :], ts_ref[p : p + 1, :]
            mid_ref[p, rows, 0:128] = re * c - im * s
            mid_ref[p, rows, 128:256] = re * s + im * c

        major_dft(load, store, scr_ref, 8, 16, -1)
        return carry

    lax.fori_loop(0, 4, forward, 0)

    sub = lax.broadcasted_iota(jnp.int32, (32, 128), 0)
    lane = lax.broadcasted_iota(jnp.int32, (32, 128), 1)
    v = me // 2 + 64 * (64 * (me % 2) + 32 * (lane // 64) + sub)
    fx = jnp.where(v < N // 2, v, v - N).astype(F32) * (1.0 / N)
    fx2 = fx * fx

    def mix(g, carry):
        p0 = g * 8
        lhs = mid_ref[pl.ds(p0, 8), :, :].reshape(256, 256)
        spec = dot3(lhs, fh_ref[...], fl_ref[...])
        parts = []
        for k in range(8):
            re, im = spec[32 * k : 32 * k + 32, 0:128], spec[32 * k : 32 * k + 32, 128:256]
            u = p0 + k + 128 * (lane % 64)
            fy = jnp.where(u < N // 2, u, u - N).astype(F32) * (1.0 / N)
            fy2 = fy * fy
            q = fx2 + fy2
            inv = 1.0 / jnp.where(q > 0, q, 1.0)
            kr = (fx2 - fy2) * inv
            ki = 2.0 * fx * fy * inv
            parts.append(jnp.concatenate([kr * re + ki * im, kr * im - ki * re], 1))
        hat = jnp.concatenate(parts, 0)
        back = dot3(hat, gh_ref[...], gl_ref[...])
        for k in range(8):
            re, im = back[32 * k : 32 * k + 32, 0:128], back[32 * k : 32 * k + 32, 128:256]
            c, s = tc_ref[pl.ds(p0 + k, 1), :], ts_ref[pl.ds(p0 + k, 1), :]
            mid_ref[p0 + k, :, 0:128] = (re * c + im * s) * (1.0 / N)
            mid_ref[p0 + k, :, 128:256] = (im * c - re * s) * (1.0 / N)
        return carry

    lax.fori_loop(0, 16, mix, 0)

    def inverse(g, carry):
        rows = pl.ds(pl.multiple_of(g * 8, 8), 8)
        rows_im = pl.ds(pl.multiple_of(g * 8 + 32, 8), 8)

        def load(i):
            return mid_ref[i, rows, 0:128], mid_ref[i, rows, 128:256]

        def store(a, value):
            re, im = value
            out_ref[a, rows, :] = re.astype(BF16)
            out_ref[a, rows_im, :] = im.astype(BF16)

        major_dft(load, store, scr_ref, 8, 16, 1)
        return carry

    lax.fori_loop(0, 4, inverse, 0)


def back_kernel(in_ref, tc_ref, ts_ref, wh_ref, wl_ref, e_ref, b_ref, scr_ref, mid_ref):
    def mix(g, carry):
        p = g * 4
        pieces = []
        for k in range(4):
            part = in_ref[pl.ds(2 * (p + k), 2), :, :].reshape(128, 128).astype(F32).T
            pieces.append(jnp.concatenate([part[0:64], part[64:128]], 1))
        lhs = jnp.concatenate(pieces, 0).astype(BF16)
        out = dot(lhs, wh_ref[...]) + dot(lhs, wl_ref[...])
        for k in range(4):
            re, im = out[64 * k : 64 * k + 64, 0:128], out[64 * k : 64 * k + 64, 128:256]
            c, s = tc_ref[pl.ds(p + k, 1), :], ts_ref[pl.ds(p + k, 1), :]
            mid_ref[p + k, :, 0:128] = re * c - im * s
            mid_ref[p + k, :, 128:256] = re * s + im * c
        return carry

    lax.fori_loop(0, 16, mix, 0)

    def row_group(g, carry):
        rows = pl.ds(pl.multiple_of(g * 8, 8), 8)

        def load(i):
            return mid_ref[i, rows, 0:128], mid_ref[i, rows, 128:256]

        def store(a, value):
            e_ref[rows, a * 128 : a * 128 + 128] = value[0]
            b_ref[rows, a * 128 : a * 128 + 128] = value[1]

        major_dft(load, store, scr_ref, 8, 8, 1)
        return carry

    lax.fori_loop(0, 8, row_group, 0)


def exchange(x):
    return lax.all_to_all(x, ("blk", "col"), split_axis=0, concat_axis=0, tiled=True)


def pack_call(pixel_row, pixel_col, strip_of_span, shear_one, shear_two, weight):
    return pl.pallas_call(
        pack_kernel,
        out_shape=jax.ShapeDtypeStruct((256, 1280), BF16),
        in_specs=[VMEM] * 6,
        out_specs=VMEM,
        name="pack",
    )(pixel_row, pixel_col, strip_of_span, shear_one, shear_two, weight)


def row_call(got):
    tags = got[:, 768].astype(F32)
    high = got[:, 1024].astype(F32)
    a = (jnp.abs(tags) - 1.0).astype(jnp.int32)
    band = a // 32
    tile = jnp.arange(256, dtype=jnp.int32) // 2 % 4
    block = tile * 16 + a % 4 + jnp.where(high >= 128.0, 4, 0) + jnp.where(tags < 0, 8, 0)
    tc, ts = twiddle_table(64, np.arange(128), -1, 1.0)
    wh, wl = split_table(row_table())
    return pl.pallas_call(
        row_kernel,
        out_shape=jax.ShapeDtypeStruct((DEV, 64, 128), BF16),
        in_specs=[SMEM, SMEM] + [VMEM] * 5,
        out_specs=VMEM,
        scratch_shapes=[
            pltpu.VMEM((3, 64, 64, 128), F32),
            pltpu.VMEM((2, 64, 8, 128), F32),
            pltpu.VMEM((64, 64, 256), F32),
        ],
        name="rows",
    )(band, block, got, tc, ts, wh, wl)


def col_call(me, x):
    tc, ts = twiddle_table(128, np.arange(128) % 64, -1, 1.0)
    fh, fl = split_table(col_table(-1))
    gh, gl = split_table(col_table(1))
    return pl.pallas_call(
        col_kernel,
        out_shape=jax.ShapeDtypeStruct((DEV, 64, 128), BF16),
        in_specs=[SMEM] + [VMEM] * 7,
        out_specs=VMEM,
        scratch_shapes=[pltpu.VMEM((2, 128, 8, 128), F32), pltpu.VMEM((128, 32, 256), F32)],
        name="columns",
    )(me, x, tc, ts, fh, fl, gh, gl)


def back_call(x):
    tc, ts = twiddle_table(64, np.arange(128), 1, 1.0 / N)
    wh, wl = split_table(row_inverse_table())
    return pl.pallas_call(
        back_kernel,
        out_shape=(jax.ShapeDtypeStruct((64, N), F32), jax.ShapeDtypeStruct((64, N), F32)),
        in_specs=[VMEM] * 5,
        out_specs=(VMEM, VMEM),
        scratch_shapes=[pltpu.VMEM((2, 64, 8, 128), F32), pltpu.VMEM((64, 64, 256), F32)],
        name="back",
    )(x, tc, ts, wh, wl)


def local(pixel_row, pixel_col, strip_of_span, shear_one, shear_two, weight):
    me = (lax.axis_index("blk") * lax.axis_size("col") + lax.axis_index("col")).reshape(1)
    sent = pack_call(pixel_row, pixel_col, strip_of_span, shear_one, shear_two, weight)
    got = exchange(sent.reshape(DEV, 2, 1280)).reshape(256, 1280)
    columns = exchange(row_call(got))
    rows = exchange(col_call(me.astype(jnp.int32), columns))
    return back_call(rows)


def solution(mesh):
    placed = (P(("blk", "col"), None),) * 6
    return jax.shard_map(
        local,
        mesh=mesh,
        in_specs=placed,
        out_specs=(P(("blk", "col"), None), P(("blk", "col"), None)),
        check_vma=False,
    )
```

time: 383 us -> 151 us (0.39); the launches traced: 376 us -> 150 us
  local copies, waits for them, and re-layouts: 110 us -> 3.57 us
  matrix products: 60.3 us -> 0 us
  other arithmetic: 55.6 us -> 0.8 us
  Pallas kernels: 0 us -> 49 us
  waiting for transfers between devices: 69.5 us -> 30.6 us
  starting transfers between devices: 21.6 us -> 3.88 us
  blocking collectives: 57.8 us -> 61.7 us
    dot_general x10 -> x0, matrix products: 60.3 us -> none  [the longest x2 16.5 us: one_group(): jnp.einsum('ckg,cgs->cks', weighted, col_hot, preferred_element_type=jnp....]
    unnamed x13 -> x4, local copies, waits for them, and re-layouts: 50.6 us -> 1.35 us
    pallas_call x0 -> x4, Pallas kernels: none -> 49 us  [the longest x1 18.7 us: row_call(): pl.pallas_call(row_kernel, out_shape=jax.ShapeDtypeStruct((DEV, 64, 128),...]
    all_to_all x3 -> x1, waiting for transfers between devices: 69.5 us -> 30.6 us  [exchange(): lax.all_to_all(x, ('blk', 'col'), split_axis=0, concat_axis=0, tiled=True)]
    reshape x4 -> x2, local copies, waits for them, and re-layouts: 31.1 us -> 2.23 us  [local(): got = exchange(sent.reshape(DEV, 2, 1280)).reshape(256, 1280)]
    all_to_all x2 -> x0, other arithmetic: 27.6 us -> none  [the longest x1 13.8 us: local(): lax.all_to_all(col_result, ('blk', 'col'), split_axis=1, concat_axis=2, t...]
    all_to_all x5 -> x0, local copies, waits for them, and re-layouts: 23.8 us -> none  [the longest x2 12 us: local(): lax.all_to_all(row_spectrum, ('blk', 'col'), split_axis=2, concat_axis=1,...]
    all_to_all x3 -> x1, starting transfers between devices: 21.6 us -> 3.88 us  [exchange(): lax.all_to_all(x, ('blk', 'col'), split_axis=0, concat_axis=0, tiled=True)]
  transfers between devices with their start and end apart: 3 -> 1, of which waited for: 3 -> 1; matrix products, arithmetic and copies ran while one was open for 2% -> 0% of each run, Pallas kernels for 0% -> 0%
where the time goes in v1:
time: 151 us; the launch traced here: 150 us
  blocking collectives  61.7 us (41%)
  Pallas kernels  49 us (32%)
  waiting for transfers between devices  30.6 us (20%)
  starting transfers between devices  3.88 us (3%)
  local copies, waits for them, and re-layouts  3.57 us (2%)
    all_to_all x2, blocking collectives, exchange(): lax.all_to_all(x, ('blk', 'col'), split_axis=0, concat_axis=0, tiled=True)  61.7 us
    all_to_all x1, waiting for transfers between devices, exchange(): lax.all_to_all(x, ('blk', 'col'), split_axis=0, concat_axis=0, tiled=True)  30.6 us
    pallas_call x1, Pallas kernels, row_call(): pl.pallas_call(row_kernel, out_shape=jax.ShapeDtypeStruct((DEV, 64, 128),...  18.7 us
    pallas_call x1, Pallas kernels, col_call(): pl.pallas_call(col_kernel, out_shape=jax.ShapeDtypeStruct((DEV, 64, 128),...  17 us
    pallas_call x1, Pallas kernels, back_call(): pl.pallas_call(back_kernel, out_shape=(jax.ShapeDtypeStruct((64, N), F32)...  10.3 us
    all_to_all x1, starting transfers between devices, exchange(): lax.all_to_all(x, ('blk', 'col'), split_axis=0, concat_axis=0, tiled=True)  3.88 us
    pallas_call x1, Pallas kernels, pack_call(): pl.pallas_call(pack_kernel, out_shape=jax.ShapeDtypeStruct((256, 1280), B...  3.06 us
  transfers between devices with their start and end apart: 1, of which 1 were waited for; matrix products, arithmetic and copies ran while one was open for 0% of the time, Pallas kernels for 0%

profile of v1, /device:TPU:1, one launch (start us, length us, event | category | flops | bytes accessed | tf_op | source)
XLA Modules:
  0.0 150.3 jit_solution(16644527879813331229)
XLA Ops:
  0.6 3.1 %pack.1 = bf16[256,1280]{1,0:T(8,128)(2,1)} custom-call(s32[256,256]{1,0:T(8,128)} %row_ref.1, s32[256,256]{1,0:T(8,128)} %col_ref.1, s32[1,256]{1,0:T(1,128)} %strip_ref.1, f32[256,256]{1,0:T(8,128)} %one_ref.1, f32[256,256]{1,0:T(8,128)} %two_ref.1, f32[256,256]{1,0:T(8,128)} %w_ref.1), custom_call_target="tpu_custom_call" | custom-call | tf_op jit(solution)/shard_map/pack/pallas_call | solution.py:325
  3.7 2.0 %reshape.30 = bf16[128,2,1280]{2,1,0:T(2,128)(2,1)S(1)} reshape(bf16[256,1280]{1,0:T(8,128)(2,1)} %pack.1) | data formatting | bytes 1310720 | tf_op jit(solution)/shard_map/reshape | solution.py:387
  5.7 26.4 %all_to_all.15 = bf16[128,2,1280]{2,1,0:T(2,128)(2,1)S(1)} all-to-all(bf16[128,2,1280]{2,1,0:T(2,128)(2,1)S(1)} %reshape.30), channel_id=1, replica_groups=mesh['blk'=32,'col'=4] {'blk','col'}, dimensions={0} | all-to-all | bytes 1310720 | tf_op jit(solution)/shard_map/all_to_all | solution.py:321
  32.1 0.2 reshape.31.in_ref
  32.4 0.0 copy-start.1
  32.4 0.2 select_reduce_fusion.1
  32.6 0.6 fusion.7
  33.2 0.0 copy-done.1
  33.2 18.7 %rows.1 = bf16[128,64,128]{2,1,0:T(8,128)(2,1)} custom-call(s32[256]{0:T(256)} %get-tuple-element.6.band_ref, s32[256]{0:T(256)} %get-tuple-element.5.block_ref, bf16[256,1280]{1,0:T(8,128)(2,1)} %copy-done.1, f32[64,128]{1,0:T(8,128)} %constant.95.clone.tc_ref, f32[64,128]{1,0:T(8,128)} %constant.96.clone.ts_ref, bf16[256,256]{1,0:T(8,128)(2,1)} %constant.97.clone.wh_ref, ...), custom_call_target="tpu_custom_call" | custom-call | tf_op jit(solution)/shard_map/rows/pallas_call | solution.py:343
  51.9 3.9 %all-to-all-start.1 = ((bf16[128,64,128]{2,1,0:T(8,128)(2,1)}), bf16[128,64,128]{2,1,0:T(8,128)(2,1)S(1)}, u32[]{:S(2)}, u32[]{:S(2)}) async-start(bf16[128,64,128]{2,1,0:T(8,128)(2,1)} %rows.1), calls=%async_computation.1 | async-start | bytes 4194304 | tf_op jit(solution)/shard_map/all_to_all | solution.py:321
  55.8 30.6 %all-to-all-done.1.in_ref = bf16[128,64,128]{2,1,0:T(8,128)(2,1)S(1)} async-done(((bf16[128,64,128]{2,1,0:T(8,128)(2,1)}), bf16[128,64,128]{2,1,0:T(8,128)(2,1)S(1)}, u32[]{:S(2)}, u32[]{:S(2)}) %all-to-all-start.1) | async-done | bytes 2097184 | tf_op jit(solution)/shard_map/all_to_all | solution.py:321
  86.4 0.0 copy-start
  86.4 1.3 copy-done
  87.8 17.0 %columns.1 = bf16[128,64,128]{2,1,0:T(8,128)(2,1)} custom-call(s32[1]{0:T(128)} %bitcast.me_ref, bf16[128,64,128]{2,1,0:T(8,128)(2,1)} %copy-done, f32[128,128]{1,0:T(8,128)} %constant.99.clone.tc_ref, f32[128,128]{1,0:T(8,128)} %constant.100.clone.ts_ref, bf16[256,256]{1,0:T(8,128)(2,1)} %constant.101.clone.fh_ref, ...), custom_call_target="tpu_custom_call" | custom-call | tf_op jit(solution)/shard_map/columns/pallas_call | solution.py:361
  104.8 35.3 %all_to_all.16.in_ref = bf16[128,64,128]{2,1,0:T(8,128)(2,1)} all-to-all(bf16[128,64,128]{2,1,0:T(8,128)(2,1)} %columns.1), channel_id=1, replica_groups=mesh['blk'=32,'col'=4] {'blk','col'}, dimensions={0} | all-to-all | bytes 4194304 | tf_op jit(solution)/shard_map/all_to_all | solution.py:321
  140.1 10.3 %back.1 = (f32[64,8192]{1,0:T(8,128)}, f32[64,8192]{1,0:T(8,128)}) custom-call(bf16[128,64,128]{2,1,0:T(8,128)(2,1)} %all_to_all.16.in_ref, f32[64,128]{1,0:T(8,128)} %constant.105.clone.tc_ref, f32[64,128]{1,0:T(8,128)} %constant.106.clone.ts_ref, bf16[256,256]{1,0:T(8,128)(2,1)} %constant.107.clone.wh_ref, bf16[256,256]{1,0:T(8,128)(2,1)} %constant.108.clone.wl_ref), custom_call_target="tpu_custom_call" | custom-call | tf_op jit(solution)/shard_map/back/pallas_call | solution.py:374
Async XLA Ops:
  32.4 0.8 copy-start.1
  51.9 34.5 %all-to-all-start.1 = ((bf16[128,64,128]{2,1,0:T(8,128)(2,1)}), bf16[128,64,128]{2,1,0:T(8,128)(2,1)S(1)}, u32[]{:S(2)}, u32[]{:S(2)}) async-start(bf16[128,64,128]{2,1,0:T(8,128)(2,1)} %rows.1), calls=%async_computation.1 | async-start | bytes 4194304 | tf_op jit(solution)/shard_map/all_to_all | solution.py:321
  86.4 1.3 copy-start

commit v2 on v1

--- a/solution.py
+++ b/solution.py
@@ -10,10 +10,13 @@
 
 N = 8192
 DEV = 128
+LIMIT = 40 << 20
 F32 = jnp.float32
 BF16 = jnp.bfloat16
+F8 = jnp.float8_e4m3fn
 VMEM = pl.BlockSpec(memory_space=pltpu.VMEM)
 SMEM = pl.BlockSpec(memory_space=pltpu.SMEM)
+HBM = pl.BlockSpec(memory_space=pl.ANY)
 
 
 def split_table(table):
@@ -148,7 +151,7 @@
         b.astype(F32).astype(BF16),
     ]
     for f in range(5):
-        out_ref[:, f * 256 : (f + 1) * 256] = dot(pick, fields[f]).astype(BF16)
+        out_ref[:, :, f * 256 : (f + 1) * 256] = dot(pick, fields[f]).astype(BF16).reshape(128, 2, 256)
 
 
 def row_kernel(
@@ -169,7 +172,7 @@
             lhs = jnp.concatenate(
                 [jnp.where(hot, data[k : k + 1, f * 256 : (f + 1) * 256], 0.0) for f in range(3)], 0
             ).astype(BF16)
-            cols = jnp.where(col128[k : k + 1] == lane_iota, 1.0, 0.0).astype(BF16)
+            cols = jnp.where(col128[k : k + 1] == lane_iota, 1.0, 0.0).astype(F8)
             part = lax.dot_general(lhs, cols, (((1,), (1,)), ((), ())), preferred_element_type=F32)
             band = pl.multiple_of(band_ref[start + k] * 8, 8)
             block = block_ref[start + k]
@@ -207,7 +210,7 @@
             out_ref[pl.ds(2 * (p + k), 2), :, :] = turned.astype(BF16).reshape(2, 64, 128)
         return carry
 
-    lax.fori_loop(0, 16, mix, 0)
+    lax.fori_loop(0, 16, mix, 0, unroll=8)
 
 
 def col_kernel(
@@ -263,7 +266,7 @@
             mid_ref[p0 + k, :, 128:256] = (im * c - re * s) * (1.0 / N)
         return carry
 
-    lax.fori_loop(0, 16, mix, 0)
+    lax.fori_loop(0, 16, mix, 0, unroll=8)
 
     def inverse(g, carry):
         rows = pl.ds(pl.multiple_of(g * 8, 8), 8)
@@ -283,7 +286,14 @@
     lax.fori_loop(0, 4, inverse, 0)
 
 
-def back_kernel(in_ref, tc_ref, ts_ref, wh_ref, wl_ref, e_ref, b_ref, scr_ref, mid_ref):
+def back_kernel(
+    in_ref, tc_ref, ts_ref, wh_ref, wl_ref, e_hbm, b_hbm, scr_ref, mid_ref, e_ref, b_ref, sems
+):
+    def leave(g, which):
+        rows = pl.ds(pl.multiple_of(g * 8, 8), 8)
+        source, target = ((e_ref, e_hbm), (b_ref, b_hbm))[which]
+        return pltpu.make_async_copy(source.at[rows], target.at[rows], sems.at[g, which])
+
     def mix(g, carry):
         p = g * 4
         pieces = []
@@ -299,7 +309,7 @@
             mid_ref[p + k, :, 128:256] = re * s + im * c
         return carry
 
-    lax.fori_loop(0, 16, mix, 0)
+    lax.fori_loop(0, 16, mix, 0, unroll=8)
 
     def row_group(g, carry):
         rows = pl.ds(pl.multiple_of(g * 8, 8), 8)
@@ -312,21 +322,31 @@
             b_ref[rows, a * 128 : a * 128 + 128] = value[1]
 
         major_dft(load, store, scr_ref, 8, 8, 1)
+        leave(g, 0).start()
+        leave(g, 1).start()
         return carry
 
     lax.fori_loop(0, 8, row_group, 0)
+    for g in range(8):
+        leave(g, 0).wait()
+        leave(g, 1).wait()
 
 
 def exchange(x):
     return lax.all_to_all(x, ("blk", "col"), split_axis=0, concat_axis=0, tiled=True)
+
+
+def on_chip(x):
+    return pltpu.with_memory_space_constraint(x, pltpu.VMEM)
 
 
 def pack_call(pixel_row, pixel_col, strip_of_span, shear_one, shear_two, weight):
     return pl.pallas_call(
         pack_kernel,
-        out_shape=jax.ShapeDtypeStruct((256, 1280), BF16),
+        out_shape=pltpu.VMEM((128, 2, 1280), BF16),
         in_specs=[VMEM] * 6,
         out_specs=VMEM,
+        compiler_params=pltpu.CompilerParams(vmem_limit_bytes=LIMIT),
         name="pack",
     )(pixel_row, pixel_col, strip_of_span, shear_one, shear_two, weight)
 
@@ -342,7 +362,7 @@
     wh, wl = split_table(row_table())
     return pl.pallas_call(
         row_kernel,
-        out_shape=jax.ShapeDtypeStruct((DEV, 64, 128), BF16),
+        out_shape=pltpu.VMEM((DEV, 64, 128), BF16),
         in_specs=[SMEM, SMEM] + [VMEM] * 5,
         out_specs=VMEM,
         scratch_shapes=[
@@ -350,6 +370,7 @@
             pltpu.VMEM((2, 64, 8, 128), F32),
             pltpu.VMEM((64, 64, 256), F32),
         ],
+        compiler_params=pltpu.CompilerParams(vmem_limit_bytes=LIMIT),
         name="rows",
     )(band, block, got, tc, ts, wh, wl)
 
@@ -360,10 +381,11 @@
     gh, gl = split_table(col_table(1))
     return pl.pallas_call(
         col_kernel,
-        out_shape=jax.ShapeDtypeStruct((DEV, 64, 128), BF16),
+        out_shape=pltpu.VMEM((DEV, 64, 128), BF16),
         in_specs=[SMEM] + [VMEM] * 7,
         out_specs=VMEM,
         scratch_shapes=[pltpu.VMEM((2, 128, 8, 128), F32), pltpu.VMEM((128, 32, 256), F32)],
+        compiler_params=pltpu.CompilerParams(vmem_limit_bytes=LIMIT),
         name="columns",
     )(me, x, tc, ts, fh, fl, gh, gl)
 
@@ -375,19 +397,27 @@
         back_kernel,
         out_shape=(jax.ShapeDtypeStruct((64, N), F32), jax.ShapeDtypeStruct((64, N), F32)),
         in_specs=[VMEM] * 5,
-        out_specs=(VMEM, VMEM),
-        scratch_shapes=[pltpu.VMEM((2, 64, 8, 128), F32), pltpu.VMEM((64, 64, 256), F32)],
+        out_specs=(HBM, HBM),
+        scratch_shapes=[
+            pltpu.VMEM((2, 64, 8, 128), F32),
+            pltpu.VMEM((64, 64, 256), F32),
+            pltpu.VMEM((64, N), F32),
+            pltpu.VMEM((64, N), F32),
+            pltpu.SemaphoreType.DMA((8, 2)),
+        ],
+        compiler_params=pltpu.CompilerParams(vmem_limit_bytes=LIMIT),
         name="back",
     )(x, tc, ts, wh, wl)
 
 
 def local(pixel_row, pixel_col, strip_of_span, shear_one, shear_two, weight):
     me = (lax.axis_index("blk") * lax.axis_size("col") + lax.axis_index("col")).reshape(1)
+    me, pixel_row = lax.optimization_barrier((me.astype(jnp.int32), pixel_row))
     sent = pack_call(pixel_row, pixel_col, strip_of_span, shear_one, shear_two, weight)
-    got = exchange(sent.reshape(DEV, 2, 1280)).reshape(256, 1280)
+    got = exchange(sent).reshape(256, 1280)
     columns = exchange(row_call(got))
-    rows = exchange(col_call(me.astype(jnp.int32), columns))
-    return back_call(rows)
+    rows = exchange(col_call(me, on_chip(columns)))
+    return back_call(on_chip(rows))
 
 
 def solution(mesh):

time: 151 us -> 127 us (0.84)
  blocking collectives: 61.7 us -> 94.8 us
  waiting for transfers between devices: 30.6 us -> 0 us
  Pallas kernels: 49 us -> 25.1 us
  starting transfers between devices: 3.88 us -> 0 us
  local copies, waits for them, and re-layouts: 3.57 us -> 5.75 us
    all_to_all x2 -> x3, blocking collectives: 61.7 us -> 94.8 us  [exchange(): lax.all_to_all(x, ('blk', 'col'), split_axis=0, concat_axis=0, tiled=True)]
    all_to_all x1 -> x0, waiting for transfers between devices: 30.6 us -> none  [exchange(): lax.all_to_all(x, ('blk', 'col'), split_axis=0, concat_axis=0, tiled=True)]
    pallas_call x3, Pallas kernels: 38.8 us -> 20.8 us  [the longest x1 11.4 us: row_call(): pl.pallas_call(row_kernel, out_shape=pltpu.VMEM((DEV, 64, 128), BF16), in...]
    pallas_call x1, Pallas kernels: 10.3 us -> 4.24 us  [back_call(): pl.pallas_call(back_kernel, out_shape=(jax.ShapeDtypeStruct((64, N), F32)...]
    unnamed x4 -> x40, local copies, waits for them, and re-layouts: 1.35 us -> 5.5 us
    all_to_all x1 -> x0, starting transfers between devices: 3.88 us -> none  [exchange(): lax.all_to_all(x, ('blk', 'col'), split_axis=0, concat_axis=0, tiled=True)]
    reshape x2 -> x1, local copies, waits for them, and re-layouts: 2.23 us -> 0.25 us  [local(): got = exchange(sent).reshape(256, 1280)]
  transfers between devices with their start and end apart: 1 -> 0, of which waited for: 1 -> 0; matrix products, arithmetic and copies ran while one was open for 0% -> 0% of each run, Pallas kernels for 0% -> 0%
where the time goes in v2:
time: 127 us
  blocking collectives  94.8 us (75%)
  Pallas kernels  25.1 us (20%)
  local copies, waits for them, and re-layouts  5.75 us (5%)
    all_to_all x3, blocking collectives, exchange(): lax.all_to_all(x, ('blk', 'col'), split_axis=0, concat_axis=0, tiled=True)  94.8 us
    pallas_call x1, Pallas kernels, row_call(): pl.pallas_call(row_kernel, out_shape=pltpu.VMEM((DEV, 64, 128), BF16), in...  11.4 us
    pallas_call x1, Pallas kernels, col_call(): pl.pallas_call(col_kernel, out_shape=pltpu.VMEM((DEV, 64, 128), BF16), in...  8.48 us
    unnamed x40, local copies, waits for them, and re-layouts  5.5 us
    pallas_call x1, Pallas kernels, back_call(): pl.pallas_call(back_kernel, out_shape=(jax.ShapeDtypeStruct((64, N), F32)...  4.24 us

profile of v2, /device:TPU:1, one launch (start us, length us, event | category | flops | bytes accessed | tf_op | source)
XLA Modules:
  0.0 126.7 jit_solution(4203547346558400531)
XLA Ops:
  0.6 0.0 copy-start
  0.6 0.9 copy-done
  1.6 0.9 copy-done.1
  2.5 0.9 copy-done.2
  3.5 0.9 copy-done.3
  4.4 0.9 copy-done.4
  5.4 0.7 copy-done.19
  6.1 1.0 pack.1
  7.1 26.4 %all_to_all.15 = bf16[128,2,1280]{2,1,0:T(2,128)(2,1)S(1)} all-to-all(bf16[128,2,1280]{2,1,0:T(2,128)(2,1)S(1)} %pack.1), channel_id=1, replica_groups=mesh['blk'=32,'col'=4] {'blk','col'}, dimensions={0} | all-to-all | bytes 1310720 | tf_op jit(solution)/shard_map/all_to_all | solution.py:336
  33.5 0.2 reshape.27.in_ref
  33.8 0.2 select_reduce_fusion.1
  34.0 11.4 %rows.1 = bf16[128,64,128]{2,1,0:T(8,128)(2,1)S(1)} custom-call(s32[256]{0:T(256)S(1)} %get-tuple-element.10.band_ref, s32[256]{0:T(256)S(1)} %get-tuple-element.9.block_ref, bf16[256,1280]{1,0:T(8,128)(2,1)S(1)} %reshape.27.in_ref, f32[64,128]{1,0:T(8,128)S(1)} %copy-done.18, f32[64,128]{1,0:T(8,128)S(1)} %copy-done.17, bf16[256,256]{1,0:T(8,128)(2,1)S(1)} %copy-done.12, ...), custom_call_target="tpu_custom_call" | custom-call | tf_op jit(solution)/shard_map/rows/pallas_call | solution.py:363
  45.4 0.0 copy-start.7
  45.4 0.0 copy-start.8
  45.4 0.0 copy-start.9
  45.4 0.0 copy-start.10
  45.5 0.0 copy-start.13
  45.5 0.0 copy-start.14
  45.5 34.2 %all_to_all.16.in_ref = bf16[128,64,128]{2,1,0:T(8,128)(2,1)S(1)} all-to-all(bf16[128,64,128]{2,1,0:T(8,128)(2,1)S(1)} %rows.1), channel_id=1, replica_groups=mesh['blk'=32,'col'=4] {'blk','col'}, dimensions={0} | all-to-all | bytes 4194304 | tf_op jit(solution)/shard_map/all_to_all | solution.py:336
  79.7 0.0 copy-done.9
  79.7 0.0 copy-done.10
  79.7 0.0 copy-done.13
  79.7 0.0 copy-done.14
  79.7 8.5 %columns.1 = bf16[128,64,128]{2,1,0:T(8,128)(2,1)S(1)} custom-call(s32[1]{0:T(128)} %bitcast.me_ref, bf16[128,64,128]{2,1,0:T(8,128)(2,1)S(1)} %all_to_all.16.in_ref, f32[128,128]{1,0:T(8,128)S(1)} %copy-done.14, f32[128,128]{1,0:T(8,128)S(1)} %copy-done.13, bf16[256,256]{1,0:T(8,128)(2,1)S(1)} %copy-done.10, bf16[256,256]{1,0:T(8,128)(2,1)S(1)} %copy-done.9, ...), custom_call_target="tpu_custom_call" | custom-call | tf_op jit(solution)/shard_map/columns/pallas_call | solution.py:382
  88.2 0.0 copy-start.5
  88.2 0.0 copy-start.6
  88.2 0.0 copy-start.15
  88.3 0.0 copy-start.16
  88.3 34.2 %all_to_all.17.in_ref = bf16[128,64,128]{2,1,0:T(8,128)(2,1)S(1)} all-to-all(bf16[128,64,128]{2,1,0:T(8,128)(2,1)S(1)} %columns.1), channel_id=1, replica_groups=mesh['blk'=32,'col'=4] {'blk','col'}, dimensions={0} | all-to-all | bytes 4194304 | tf_op jit(solution)/shard_map/all_to_all | solution.py:336
  122.4 0.0 copy-done.5
  122.4 0.0 copy-done.15
  122.5 4.2 %back.1 = (f32[64,8192]{1,0:T(8,128)}, f32[64,8192]{1,0:T(8,128)}) custom-call(bf16[128,64,128]{2,1,0:T(8,128)(2,1)S(1)} %all_to_all.17.in_ref, f32[64,128]{1,0:T(8,128)S(1)} %copy-done.16, f32[64,128]{1,0:T(8,128)S(1)} %copy-done.15, bf16[256,256]{1,0:T(8,128)(2,1)S(1)} %copy-done.6, bf16[256,256]{1,0:T(8,128)(2,1)S(1)} %copy-done.5), custom_call_target="tpu_custom_call" | custom-call | tf_op jit(solution)/shard_map/back/pallas_call | solution.py:396
  (18 shorter events, 0.0 us)
Async XLA Ops:
  0.6 1.0 copy-start
  1.6 0.9 copy-start.1
  2.5 0.9 copy-start.2
  3.5 0.9 copy-start.3
  4.4 0.9 copy-start.4
  5.4 0.7 copy-start.19
  6.1 27.9 %copy-start.11 = (bf16[256,256]{1,0:T(8,128)(2,1)S(1)}, bf16[256,256]{1,0:T(8,128)(2,1)}, u32[]{:S(2)}) copy-start(bf16[256,256]{1,0:T(8,128)(2,1)} %constant.98.clone.wl_ref) | copy-start | bytes 393220
  6.1 27.9 %copy-start.12 = (bf16[256,256]{1,0:T(8,128)(2,1)S(1)}, bf16[256,256]{1,0:T(8,128)(2,1)}, u32[]{:S(2)}) copy-start(bf16[256,256]{1,0:T(8,128)(2,1)} %constant.97.clone.wh_ref) | copy-start | bytes 393220
  6.1 27.9 %copy-start.17 = (f32[64,128]{1,0:T(8,128)S(1)}, f32[64,128]{1,0:T(8,128)}, u32[]{:S(2)}) copy-start(f32[64,128]{1,0:T(8,128)} %constant.96.clone.ts_ref) | copy-start | bytes 98308
  6.1 27.9 %copy-start.18 = (f32[64,128]{1,0:T(8,128)S(1)}, f32[64,128]{1,0:T(8,128)}, u32[]{:S(2)}) copy-start(f32[64,128]{1,0:T(8,128)} %constant.95.clone.tc_ref) | copy-start | bytes 98308
  45.4 34.3 %copy-start.7 = (bf16[256,256]{1,0:T(8,128)(2,1)S(1)}, bf16[256,256]{1,0:T(8,128)(2,1)}, u32[]{:S(2)}) copy-start(bf16[256,256]{1,0:T(8,128)(2,1)} %constant.104.clone.gl_ref) | copy-start | bytes 393220
  45.4 34.3 %copy-start.8 = (bf16[256,256]{1,0:T(8,128)(2,1)S(1)}, bf16[256,256]{1,0:T(8,128)(2,1)}, u32[]{:S(2)}) copy-start(bf16[256,256]{1,0:T(8,128)(2,1)} %constant.103.clone.gh_ref) | copy-start | bytes 393220
  45.4 34.3 %copy-start.9 = (bf16[256,256]{1,0:T(8,128)(2,1)S(1)}, bf16[256,256]{1,0:T(8,128)(2,1)}, u32[]{:S(2)}) copy-start(bf16[256,256]{1,0:T(8,128)(2,1)} %constant.102.clone.fl_ref) | copy-start | bytes 393220
  45.4 34.3 %copy-start.10 = (bf16[256,256]{1,0:T(8,128)(2,1)S(1)}, bf16[256,256]{1,0:T(8,128)(2,1)}, u32[]{:S(2)}) copy-start(bf16[256,256]{1,0:T(8,128)(2,1)} %constant.101.clone.fh_ref) | copy-start | bytes 393220
  45.5 34.3 %copy-start.13 = (f32[128,128]{1,0:T(8,128)S(1)}, f32[128,128]{1,0:T(8,128)}, u32[]{:S(2)}) copy-start(f32[128,128]{1,0:T(8,128)} %constant.100.clone.ts_ref) | copy-start | bytes 196612
  45.5 34.3 %copy-start.14 = (f32[128,128]{1,0:T(8,128)S(1)}, f32[128,128]{1,0:T(8,128)}, u32[]{:S(2)}) copy-start(f32[128,128]{1,0:T(8,128)} %constant.99.clone.tc_ref) | copy-start | bytes 196612
  88.2 34.2 %copy-start.5 = (bf16[256,256]{1,0:T(8,128)(2,1)S(1)}, bf16[256,256]{1,0:T(8,128)(2,1)}, u32[]{:S(2)}) copy-start(bf16[256,256]{1,0:T(8,128)(2,1)} %constant.108.clone.wl_ref) | copy-start | bytes 393220
  88.2 34.2 %copy-start.6 = (bf16[256,256]{1,0:T(8,128)(2,1)S(1)}, bf16[256,256]{1,0:T(8,128)(2,1)}, u32[]{:S(2)}) copy-start(bf16[256,256]{1,0:T(8,128)(2,1)} %constant.107.clone.wh_ref) | copy-start | bytes 393220
  88.2 34.2 %copy-start.15 = (f32[64,128]{1,0:T(8,128)S(1)}, f32[64,128]{1,0:T(8,128)}, u32[]{:S(2)}) copy-start(f32[64,128]{1,0:T(8,128)} %constant.106.clone.ts_ref) | copy-start | bytes 98308
  88.3 34.2 %copy-start.16 = (f32[64,128]{1,0:T(8,128)S(1)}, f32[64,128]{1,0:T(8,128)}, u32[]{:S(2)}) copy-start(f32[64,128]{1,0:T(8,128)} %constant.105.clone.tc_ref) | copy-start | bytes 98308

commit v3 on v2

--- a/solution.py
+++ b/solution.py
@@ -13,10 +13,9 @@
 LIMIT = 40 << 20
 F32 = jnp.float32
 BF16 = jnp.bfloat16
-F8 = jnp.float8_e4m3fn
 VMEM = pl.BlockSpec(memory_space=pltpu.VMEM)
 SMEM = pl.BlockSpec(memory_space=pltpu.SMEM)
-HBM = pl.BlockSpec(memory_space=pl.ANY)
+HBM = pl.BlockSpec(memory_space=pltpu.HBM)
 
 
 def split_table(table):
@@ -128,7 +127,25 @@
     return dot(xh, high) + dot(xl, high) + dot(xh, low)
 
 
-def pack_kernel(row_ref, col_ref, strip_ref, one_ref, two_ref, w_ref, out_ref):
+def pack_kernel(
+    row_hbm, col_hbm, strip_hbm, one_hbm, two_hbm, w_hbm, out_ref, strip_ref, ints_ref, floats_ref, sems
+):
+    copies = [
+        pltpu.make_async_copy(source, target, sems.at[i])
+        for i, (source, target) in enumerate(
+            [
+                (strip_hbm, strip_ref),
+                (w_hbm, floats_ref.at[0]),
+                (one_hbm, floats_ref.at[1]),
+                (two_hbm, floats_ref.at[2]),
+                (row_hbm, ints_ref.at[0]),
+                (col_hbm, ints_ref.at[1]),
+            ]
+        )
+    ]
+    for copy in copies:
+        copy.start()
+    copies[0].wait()
     strip = strip_ref[...].astype(F32)
     along = jnp.broadcast_to(strip, (256, 256))
     down = along.T
@@ -137,50 +154,69 @@
     earlier = jnp.where((along == down) & (i < j), 1.0, 0.0)
     place = 2.0 * strip + jnp.sum(earlier, axis=0, keepdims=True)
     pick = (place.astype(jnp.int32) == i).astype(BF16)
-    w = w_ref[...]
-    row = row_ref[...]
-    col = col_ref[...]
+
+    def send(f, field):
+        moved = dot(pick, field.astype(BF16)).astype(BF16)
+        out_ref[:, :, f * 256 : (f + 1) * 256] = moved.reshape(128, 2, 256)
+
+    copies[1].wait()
+    w = floats_ref[0]
+    send(0, w)
+    copies[2].wait()
+    send(1, w * floats_ref[1])
+    copies[3].wait()
+    send(2, w * floats_ref[2])
+    copies[4].wait()
+    copies[5].wait()
+    row = ints_ref[0]
+    col = ints_ref[1]
     block = col // 128
     a = (row * 4 + block % 4 + 1) * jnp.where(block >= 8, -1, 1)
     b = col % 128 + 128 * (block // 4 % 2)
-    fields = [
-        w.astype(BF16),
-        (w * one_ref[...]).astype(BF16),
-        (w * two_ref[...]).astype(BF16),
-        a.astype(F32).astype(BF16),
-        b.astype(F32).astype(BF16),
-    ]
-    for f in range(5):
-        out_ref[:, :, f * 256 : (f + 1) * 256] = dot(pick, fields[f]).astype(BF16).reshape(128, 2, 256)
+    send(3, a.astype(F32))
+    send(4, b.astype(F32))
 
 
 def row_kernel(
     band_ref, block_ref, in_ref, tc_ref, ts_ref, wh_ref, wl_ref, out_ref, acc_ref, scr_ref, mid_ref
 ):
     acc_ref[...] = jnp.zeros_like(acc_ref)
-    lane_iota = lax.broadcasted_iota(jnp.int32, (128, 256), 0)
-    row_iota = lax.broadcasted_iota(jnp.int32, (8, 256), 0)
+    lane_iota = lax.broadcasted_iota(jnp.int32, (64, 256), 0).astype(F32).astype(BF16)
+    row_iota = lax.broadcasted_iota(jnp.int32, (16, 256), 0).astype(F32).astype(BF16)
+    one = jnp.ones((), BF16)
+    none = jnp.zeros((), BF16)
 
     def bin_group(g, carry):
         start = pl.multiple_of(g * 16, 16)
-        data = in_ref[pl.ds(start, 16), :].astype(F32)
-        a = (jnp.abs(data[:, 768:1024]) - 1.0).astype(jnp.int32)
-        row8 = (a >> 2) & 7
-        col128 = data[:, 1024:1280].astype(jnp.int32) & 127
+        data = in_ref[pl.ds(start, 16), 0:768]
+        tags = in_ref[pl.ds(start, 16), 768:1280].astype(F32)
+        a = (jnp.abs(tags[:, 0:256]) - 1.0).astype(jnp.int32)
+        b = tags[:, 256:512].astype(jnp.int32)
+        high = (((a >> 2) & 7) + ((b >> 3) & 8)).astype(F32).astype(BF16)
+        low = (b & 63).astype(F32).astype(BF16)
         for k in range(16):
-            hot = row8[k : k + 1] == row_iota
+            hot = jnp.broadcast_to(high[k : k + 1], (16, 256)) == row_iota
             lhs = jnp.concatenate(
-                [jnp.where(hot, data[k : k + 1, f * 256 : (f + 1) * 256], 0.0) for f in range(3)], 0
-            ).astype(BF16)
-            cols = jnp.where(col128[k : k + 1] == lane_iota, 1.0, 0.0).astype(F8)
+                [
+                    jnp.where(
+                        hot,
+                        jnp.broadcast_to(data[k : k + 1, f * 256 : (f + 1) * 256], (16, 256)),
+                        none,
+                    )
+                    for f in range(3)
+                ],
+                0,
+            )
+            cols = jnp.where(jnp.broadcast_to(low[k : k + 1], (64, 256)) == lane_iota, one, none)
             part = lax.dot_general(lhs, cols, (((1,), (1,)), ((), ())), preferred_element_type=F32)
             band = pl.multiple_of(band_ref[start + k] * 8, 8)
             block = block_ref[start + k]
             for f in range(3):
-                acc_ref[f, block, pl.ds(band, 8), :] += part[f * 8 : f * 8 + 8]
-        return carry
-
-    lax.fori_loop(0, 16, bin_group, 0)
+                both = [part[f * 16 : f * 16 + 8], part[f * 16 + 8 : f * 16 + 16]]
+                acc_ref[f, block, pl.ds(band, 8), :] += jnp.concatenate(both, 1)
+        return carry
+
+    lax.fori_loop(0, 16, bin_group, 0, unroll=8)
 
     def row_group(g, carry):
         rows = pl.ds(pl.multiple_of(g * 8, 8), 8)
@@ -210,7 +246,7 @@
             out_ref[pl.ds(2 * (p + k), 2), :, :] = turned.astype(BF16).reshape(2, 64, 128)
         return carry
 
-    lax.fori_loop(0, 16, mix, 0, unroll=8)
+    lax.fori_loop(0, 16, mix, 0, unroll=16)
 
 
 def col_kernel(
@@ -238,9 +274,11 @@
 
     sub = lax.broadcasted_iota(jnp.int32, (32, 128), 0)
     lane = lax.broadcasted_iota(jnp.int32, (32, 128), 1)
+    line = lax.broadcasted_iota(jnp.int32, (1, 128), 1)
     v = me // 2 + 64 * (64 * (me % 2) + 32 * (lane // 64) + sub)
     fx = jnp.where(v < N // 2, v, v - N).astype(F32) * (1.0 / N)
     fx2 = fx * fx
+    twice = 2.0 * fx
 
     def mix(g, carry):
         p0 = g * 8
@@ -249,13 +287,13 @@
         parts = []
         for k in range(8):
             re, im = spec[32 * k : 32 * k + 32, 0:128], spec[32 * k : 32 * k + 32, 128:256]
-            u = p0 + k + 128 * (lane % 64)
+            u = p0 + k + 128 * (line % 64)
             fy = jnp.where(u < N // 2, u, u - N).astype(F32) * (1.0 / N)
             fy2 = fy * fy
             q = fx2 + fy2
             inv = 1.0 / jnp.where(q > 0, q, 1.0)
             kr = (fx2 - fy2) * inv
-            ki = 2.0 * fx * fy * inv
+            ki = twice * fy * inv
             parts.append(jnp.concatenate([kr * re + ki * im, kr * im - ki * re], 1))
         hat = jnp.concatenate(parts, 0)
         back = dot3(hat, gh_ref[...], gl_ref[...])
@@ -266,7 +304,7 @@
             mid_ref[p0 + k, :, 128:256] = (im * c - re * s) * (1.0 / N)
         return carry
 
-    lax.fori_loop(0, 16, mix, 0, unroll=8)
+    lax.fori_loop(0, 16, mix, 0, unroll=16)
 
     def inverse(g, carry):
         rows = pl.ds(pl.multiple_of(g * 8, 8), 8)
@@ -309,7 +347,7 @@
             mid_ref[p + k, :, 128:256] = re * s + im * c
         return carry
 
-    lax.fori_loop(0, 16, mix, 0, unroll=8)
+    lax.fori_loop(0, 16, mix, 0, unroll=16)
 
     def row_group(g, carry):
         rows = pl.ds(pl.multiple_of(g * 8, 8), 8)
@@ -340,15 +378,21 @@
     return pltpu.with_memory_space_constraint(x, pltpu.VMEM)
 
 
-def pack_call(pixel_row, pixel_col, strip_of_span, shear_one, shear_two, weight):
+def pack_call(*args):
     return pl.pallas_call(
         pack_kernel,
         out_shape=pltpu.VMEM((128, 2, 1280), BF16),
-        in_specs=[VMEM] * 6,
+        in_specs=[HBM] * 6,
         out_specs=VMEM,
+        scratch_shapes=[
+            pltpu.VMEM((1, 256), jnp.int32),
+            pltpu.VMEM((2, 256, 256), jnp.int32),
+            pltpu.VMEM((3, 256, 256), F32),
+            pltpu.SemaphoreType.DMA((6,)),
+        ],
         compiler_params=pltpu.CompilerParams(vmem_limit_bytes=LIMIT),
         name="pack",
-    )(pixel_row, pixel_col, strip_of_span, shear_one, shear_two, weight)
+    )(*(pltpu.with_memory_space_constraint(x, pltpu.HBM) for x in args))
 
 
 def row_call(got):

time: 127 us -> 119 us (0.937)
  local copies, waits for them, and re-layouts: 5.75 us -> 0.34 us
  Pallas kernels: 25.1 us -> 22.7 us
    unnamed x40 -> x28, local copies, waits for them, and re-layouts: 5.5 us -> 0.1 us
    pallas_call x1, Pallas kernels: 11.4 us -> 8.05 us  [row_call(): pl.pallas_call(row_kernel, out_shape=pltpu.VMEM((DEV, 64, 128), BF16), in...]
    pallas_call x1, Pallas kernels: 0.97 us -> 2.51 us  [pack_call(): pl.pallas_call(pack_kernel, out_shape=pltpu.VMEM((128, 2, 1280), BF16), i...]
where the time goes in v3:
time: 119 us
  blocking collectives  94.8 us (80%)
  Pallas kernels  22.7 us (19%)
    all_to_all x3, blocking collectives, exchange(): lax.all_to_all(x, ('blk', 'col'), split_axis=0, concat_axis=0, tiled=True)  94.8 us
    pallas_call x1, Pallas kernels, col_call(): pl.pallas_call(col_kernel, out_shape=pltpu.VMEM((DEV, 64, 128), BF16), in...  8.09 us
    pallas_call x1, Pallas kernels, row_call(): pl.pallas_call(row_kernel, out_shape=pltpu.VMEM((DEV, 64, 128), BF16), in...  8.05 us
    pallas_call x1, Pallas kernels, back_call(): pl.pallas_call(back_kernel, out_shape=(jax.ShapeDtypeStruct((64, N), F32)...  4 us
    pallas_call x1, Pallas kernels, pack_call(): pl.pallas_call(pack_kernel, out_shape=pltpu.VMEM((128, 2, 1280), BF16), i...  2.51 us

profile of v3, /device:TPU:1, one launch (start us, length us, event | category | flops | bytes accessed | tf_op | source)
XLA Modules:
  0.0 118.9 jit_solution(17613404109837972799)
XLA Ops:
  0.6 0.0 copy-start.6
  0.7 0.0 copy-start.7
  0.7 0.0 copy-start.12
  0.7 0.0 copy-start.13
  0.7 2.5 %pack.1 = bf16[128,2,1280]{2,1,0:T(2,128)(2,1)S(1)} custom-call(s32[256,256]{1,0:T(8,128)} %row_hbm, s32[256,256]{1,0:T(8,128)} %col_hbm.1, s32[1,256]{1,0:T(1,128)} %strip_hbm.1, f32[256,256]{1,0:T(8,128)} %one_hbm.1, f32[256,256]{1,0:T(8,128)} %two_hbm.1, f32[256,256]{1,0:T(8,128)} %w_hbm.1), custom_call_target="tpu_custom_call" | custom-call | tf_op jit(solution)/shard_map/pack/pallas_call | solution.py:382
  3.2 26.4 %all_to_all.15 = bf16[128,2,1280]{2,1,0:T(2,128)(2,1)S(1)} all-to-all(bf16[128,2,1280]{2,1,0:T(2,128)(2,1)S(1)} %pack.1), channel_id=1, replica_groups=mesh['blk'=32,'col'=4] {'blk','col'}, dimensions={0} | all-to-all | bytes 1310720 | tf_op jit(solution)/shard_map/all_to_all | solution.py:374
  29.7 0.2 reshape.27.in_ref
  29.9 0.2 select_reduce_fusion.1
  30.1 0.0 copy-done.6
  30.1 0.0 copy-done.7
  30.1 0.0 copy-done.12
  30.1 0.0 copy-done.13
  30.2 8.0 %rows.1 = bf16[128,64,128]{2,1,0:T(8,128)(2,1)S(1)} custom-call(s32[256]{0:T(256)S(1)} %get-tuple-element.10.band_ref, s32[256]{0:T(256)S(1)} %get-tuple-element.9.block_ref, bf16[256,1280]{1,0:T(8,128)(2,1)S(1)} %reshape.27.in_ref, f32[64,128]{1,0:T(8,128)S(1)} %copy-done.13, f32[64,128]{1,0:T(8,128)S(1)} %copy-done.12, bf16[256,256]{1,0:T(8,128)(2,1)S(1)} %copy-done.7, ...), custom_call_target="tpu_custom_call" | custom-call | tf_op jit(solution)/shard_map/rows/pallas_call | solution.py:407
  38.2 0.0 copy-start.2
  38.2 0.0 copy-start.3
  38.2 0.0 copy-start.4
  38.2 0.0 copy-start.5
  38.3 0.0 copy-start.8
  38.3 0.0 copy-start.9
  38.3 34.2 %all_to_all.16.in_ref = bf16[128,64,128]{2,1,0:T(8,128)(2,1)S(1)} all-to-all(bf16[128,64,128]{2,1,0:T(8,128)(2,1)S(1)} %rows.1), channel_id=1, replica_groups=mesh['blk'=32,'col'=4] {'blk','col'}, dimensions={0} | all-to-all | bytes 4194304 | tf_op jit(solution)/shard_map/all_to_all | solution.py:374
  72.5 0.0 copy-done.2
  72.5 0.0 copy-done.3
  72.5 0.0 copy-done.4
  72.5 8.1 %columns.1 = bf16[128,64,128]{2,1,0:T(8,128)(2,1)S(1)} custom-call(s32[1]{0:T(128)} %bitcast.me_ref, bf16[128,64,128]{2,1,0:T(8,128)(2,1)S(1)} %all_to_all.16.in_ref, f32[128,128]{1,0:T(8,128)S(1)} %copy-done.9, f32[128,128]{1,0:T(8,128)S(1)} %copy-done.8, bf16[256,256]{1,0:T(8,128)(2,1)S(1)} %copy-done.5, bf16[256,256]{1,0:T(8,128)(2,1)S(1)} %copy-done.4, ...), custom_call_target="tpu_custom_call" | custom-call | tf_op jit(solution)/shard_map/columns/pallas_call | solution.py:426
  80.6 0.0 copy-start
  80.6 0.0 copy-start.1
  80.7 0.0 copy-start.10
  80.7 0.0 copy-start.11
  80.7 34.2 %all_to_all.17.in_ref = bf16[128,64,128]{2,1,0:T(8,128)(2,1)S(1)} all-to-all(bf16[128,64,128]{2,1,0:T(8,128)(2,1)S(1)} %columns.1), channel_id=1, replica_groups=mesh['blk'=32,'col'=4] {'blk','col'}, dimensions={0} | all-to-all | bytes 4194304 | tf_op jit(solution)/shard_map/all_to_all | solution.py:374
  114.9 0.0 copy-done.10
  114.9 0.0 copy-done.11
  114.9 4.0 %back.1 = (f32[64,8192]{1,0:T(8,128)}, f32[64,8192]{1,0:T(8,128)}) custom-call(bf16[128,64,128]{2,1,0:T(8,128)(2,1)S(1)} %all_to_all.17.in_ref, f32[64,128]{1,0:T(8,128)S(1)} %copy-done.11, f32[64,128]{1,0:T(8,128)S(1)} %copy-done.10, bf16[256,256]{1,0:T(8,128)(2,1)S(1)} %copy-done.1, bf16[256,256]{1,0:T(8,128)(2,1)S(1)} %copy-done), custom_call_target="tpu_custom_call" | custom-call | tf_op jit(solution)/shard_map/back/pallas_call | solution.py:440
  (6 shorter events, 0.0 us)
Async XLA Ops:
  0.6 29.5 %copy-start.6 = (bf16[256,256]{1,0:T(8,128)(2,1)S(1)}, bf16[256,256]{1,0:T(8,128)(2,1)}, u32[]{:S(2)}) copy-start(bf16[256,256]{1,0:T(8,128)(2,1)} %constant.98.clone.wl_ref) | copy-start | bytes 393220
  0.7 29.5 %copy-start.7 = (bf16[256,256]{1,0:T(8,128)(2,1)S(1)}, bf16[256,256]{1,0:T(8,128)(2,1)}, u32[]{:S(2)}) copy-start(bf16[256,256]{1,0:T(8,128)(2,1)} %constant.97.clone.wh_ref) | copy-start | bytes 393220
  0.7 29.5 %copy-start.12 = (f32[64,128]{1,0:T(8,128)S(1)}, f32[64,128]{1,0:T(8,128)}, u32[]{:S(2)}) copy-start(f32[64,128]{1,0:T(8,128)} %constant.96.clone.ts_ref) | copy-start | bytes 98308
  0.7 29.5 %copy-start.13 = (f32[64,128]{1,0:T(8,128)S(1)}, f32[64,128]{1,0:T(8,128)}, u32[]{:S(2)}) copy-start(f32[64,128]{1,0:T(8,128)} %constant.95.clone.tc_ref) | copy-start | bytes 98308
  38.2 34.3 %copy-start.2 = (bf16[256,256]{1,0:T(8,128)(2,1)S(1)}, bf16[256,256]{1,0:T(8,128)(2,1)}, u32[]{:S(2)}) copy-start(bf16[256,256]{1,0:T(8,128)(2,1)} %constant.104.clone.gl_ref) | copy-start | bytes 393220
  38.2 34.3 %copy-start.3 = (bf16[256,256]{1,0:T(8,128)(2,1)S(1)}, bf16[256,256]{1,0:T(8,128)(2,1)}, u32[]{:S(2)}) copy-start(bf16[256,256]{1,0:T(8,128)(2,1)} %constant.103.clone.gh_ref) | copy-start | bytes 393220
  38.2 34.3 %copy-start.4 = (bf16[256,256]{1,0:T(8,128)(2,1)S(1)}, bf16[256,256]{1,0:T(8,128)(2,1)}, u32[]{:S(2)}) copy-start(bf16[256,256]{1,0:T(8,128)(2,1)} %constant.102.clone.fl_ref) | copy-start | bytes 393220
  38.2 34.3 %copy-start.5 = (bf16[256,256]{1,0:T(8,128)(2,1)S(1)}, bf16[256,256]{1,0:T(8,128)(2,1)}, u32[]{:S(2)}) copy-start(bf16[256,256]{1,0:T(8,128)(2,1)} %constant.101.clone.fh_ref) | copy-start | bytes 393220
  38.3 34.3 %copy-start.8 = (f32[128,128]{1,0:T(8,128)S(1)}, f32[128,128]{1,0:T(8,128)}, u32[]{:S(2)}) copy-start(f32[128,128]{1,0:T(8,128)} %constant.100.clone.ts_ref) | copy-start | bytes 196612
  38.3 34.3 %copy-start.9 = (f32[128,128]{1,0:T(8,128)S(1)}, f32[128,128]{1,0:T(8,128)}, u32[]{:S(2)}) copy-start(f32[128,128]{1,0:T(8,128)} %constant.99.clone.tc_ref) | copy-start | bytes 196612
  80.6 34.2 %copy-start = (bf16[256,256]{1,0:T(8,128)(2,1)S(1)}, bf16[256,256]{1,0:T(8,128)(2,1)}, u32[]{:S(2)}) copy-start(bf16[256,256]{1,0:T(8,128)(2,1)} %constant.108.clone.wl_ref) | copy-start | bytes 393220
  80.6 34.2 %copy-start.1 = (bf16[256,256]{1,0:T(8,128)(2,1)S(1)}, bf16[256,256]{1,0:T(8,128)(2,1)}, u32[]{:S(2)}) copy-start(bf16[256,256]{1,0:T(8,128)(2,1)} %constant.107.clone.wh_ref) | copy-start | bytes 393220
  80.7 34.2 %copy-start.10 = (f32[64,128]{1,0:T(8,128)S(1)}, f32[64,128]{1,0:T(8,128)}, u32[]{:S(2)}) copy-start(f32[64,128]{1,0:T(8,128)} %constant.106.clone.ts_ref) | copy-start | bytes 98308
  80.7 34.2 %copy-start.11 = (f32[64,128]{1,0:T(8,128)S(1)}, f32[64,128]{1,0:T(8,128)}, u32[]{:S(2)}) copy-start(f32[64,128]{1,0:T(8,128)} %constant.105.clone.tc_ref) | copy-start | bytes 98308
